TPU v7x, 768 devices: a whole 4x8x12 slice. The times are simulated.
768 devices in a mesh: section: 32 (over y, z_hi), tensor: 4 (over x), dp: 6 (over z_lo, core).
Axes of the slice: x: 4, y: 8, z: 12 (z_hi: 4, z_lo: 3; z = z_hi * 3 + z_lo), core: 2. Of those that a mesh axis runs over, the one named last changes fastest.
Arguments:
- forward_rows: bfloat16 [32, 6, 192, 8192], P('section', 'dp', None, 'tensor'), may hold values from -6 to 6
- saved_rows: bfloat16 [32, 6, 192, 8192], P('section', 'dp', None, 'tensor'), may hold values from -40.5 to 40.5
- output_grad: bfloat16 [32, 6, 192, 8192], P('section', 'dp', None, 'tensor'), may hold values from -1.27 to 1.27
- lengths: int32 [32, 6, 2], P('section', 'dp'), may hold values from 1 to 96
- norm_gain: bfloat16 [32, 8192], P('section', 'tensor'), may hold values from 0.5 to 1.5
- down_map: bfloat16 [32, 192, 8192], P('section', None, 'tensor'), may hold values from -0.067396115 to 0.067396115
- up_map: bfloat16 [32, 192, 8192], P('section', None, 'tensor'), may hold values from -1.0625 to 1.0625
Outputs:
- next_inputs: bfloat16 [32, 6, 192, 8192], P('section', 'dp', None, 'tensor')
- next_grads: bfloat16 [32, 6, 192, 8192], P('section', 'dp', None, 'tensor')
- grad_down: bfloat16 [32, 192, 8192], P('section', 'dp', 'tensor')
- grad_up: bfloat16 [32, 192, 8192], P('section', 'dp', 'tensor')
All inputs are finite; a program needn't handle non-finite values.
Results may differ from a plain program's by a relative error of at most 0.02.
Values may be sent and summed in bfloat16 or wider, within the bound.
A program may use at most 32 MiB of HBM per device.

v0:
```python
import jax
import jax.numpy as jnp
from jax import lax
from jax.sharding import PartitionSpec as P

EPSILON = 1e-05


def split_up(shard, dim, devices):
    lengths = shard.shape
    pieces = shard.reshape(*lengths[:dim], devices, lengths[dim] // devices, *lengths[dim + 1 :])
    return jnp.moveaxis(pieces, dim, 0)


def summed_on_arrival(shard, axis, dim):
    pieces = split_up(shard, dim, lax.axis_size(axis))
    arrived = lax.all_to_all(pieces, axis, split_axis=0, concat_axis=0, tiled=True)
    return arrived.astype(jnp.float32).sum(axis=0)


def in_one_piece(arrays, axis, dim, along):
    both = jnp.concatenate(arrays, axis=along)
    out, at, finished = (summed_on_arrival(both, axis, dim), 0, [])
    for a in arrays:
        finished.append(lax.slice_in_dim(out, at, at + a.shape[along], axis=along))
        at += a.shape[along]
    return tuple(finished)


def sent_to_all(shard, axis):
    copies = jnp.broadcast_to(shard, (lax.axis_size(axis), *shard.shape))
    return lax.all_to_all(copies, axis, split_axis=0, concat_axis=0, tiled=True)


def laid_out(pieces, dim):
    lengths = list(pieces.shape[1:])
    lengths[dim] *= pieces.shape[0]
    return jnp.moveaxis(pieces, 0, dim).reshape(lengths)


def gathered_copies(shard, axis, dim):
    pieces = sent_to_all(shard, axis)
    return laid_out(pieces, dim)


def in_one_piece_2(arrays, axis, dim, along):
    both = jnp.concatenate(arrays, axis=along)
    out, at, finished = (gathered_copies(both, axis, dim), 0, [])
    for a in arrays:
        finished.append(lax.slice_in_dim(out, at, at + a.shape[along], axis=along))
        at += a.shape[along]
    return tuple(finished)


def padded_2(cells, sides, width):
    for axis, dim in sides:
        count = lax.axis_size(axis)
        ends = count - 1
        head = lax.slice_in_dim(cells, 0, width, axis=dim)
        tail = lax.slice_in_dim(cells, cells.shape[dim] - width, cells.shape[dim], axis=dim)
        cells = jnp.concatenate(
            [
                lax.ppermute(tail, axis, [(i, (i + 1) % count) for i in range(ends)]),
                cells,
                lax.ppermute(head, axis, [((i + 1) % count, i) for i in range(ends)]),
            ],
            axis=dim,
        )
    return cells


def contract_last(left_side, right_side):
    return lax.dot_general(
        left_side, right_side, (((1,), (1,)), ((), ())), preferred_element_type=jnp.float32
    )


def contract_rows(left_side, right_side):
    return lax.dot_general(
        left_side, right_side, (((0,), (0,)), ((), ())), preferred_element_type=jnp.float32
    )


def silu_slope(values):
    gate_value = jax.nn.sigmoid(values)
    return gate_value * (1.0 + values * (1.0 - gate_value))


def shards(forward_rows, saved_rows, output_grad, lengths, norm_gain, down_map, up_map):
    forward_block = forward_rows[0, 0]
    saved_block = saved_rows[0, 0]
    incoming = output_grad[0, 0]
    seq_lengths = lengths[0, 0]
    gain_cols = norm_gain[0].astype(jnp.float32)
    down_cols = down_map[0]
    up_cols = up_map[0]
    row_count = forward_block.shape[0]
    seq_rows = row_count // 2
    full_width = forward_block.shape[1] * lax.axis_size("tensor")
    forward_values = forward_block.astype(jnp.float32)
    saved_values = saved_block.astype(jnp.float32)
    forward_total, saved_total = lax.psum(
        (
            jnp.sum(forward_values * forward_values, axis=1),
            jnp.sum(saved_values * saved_values, axis=1),
        ),
        "tensor",
    )
    forward_scale = lax.rsqrt(forward_total / full_width + EPSILON)[:, None]
    saved_scale = lax.rsqrt(saved_total / full_width + EPSILON)[:, None]
    forward_normed = (forward_values * forward_scale * gain_cols).astype(jnp.bfloat16)
    saved_normed = (saved_values * saved_scale * gain_cols).astype(jnp.bfloat16)
    position = jnp.arange(row_count, dtype=jnp.int32)
    length_limit = jnp.where(position // seq_rows == 0, seq_lengths[0], seq_lengths[1])
    keep_rows = position % seq_rows < length_limit
    kept_grad = jnp.where(keep_rows[:, None], incoming, jnp.zeros_like(incoming))
    forward_part = contract_last(forward_normed, down_cols)
    saved_part = contract_last(saved_normed, down_cols)
    slope_part = contract_last(kept_grad, up_cols)
    forward_share, saved_share, slope_share = in_one_piece(
        (
            forward_part.astype(jnp.bfloat16),
            saved_part.astype(jnp.bfloat16),
            slope_part.astype(jnp.bfloat16),
        ),
        "tensor",
        1,
        0,
    )
    forward_act, saved_act, back_rank = in_one_piece_2(
        (
            jax.nn.silu(forward_share).astype(jnp.bfloat16),
            jax.nn.silu(saved_share).astype(jnp.bfloat16),
            (slope_share * silu_slope(saved_share)).astype(jnp.bfloat16),
        ),
        "tensor",
        1,
        0,
    )
    forward_out = (
        forward_values + jnp.dot(forward_act, up_cols, preferred_element_type=jnp.float32)
    ).astype(jnp.bfloat16)
    back_normed = jnp.dot(back_rank, down_cols, preferred_element_type=jnp.float32)
    weighted = gain_cols * back_normed
    correction = lax.psum(jnp.sum(saved_values * weighted, axis=1), "tensor")[:, None] / full_width
    scale_cube = saved_scale * saved_scale * saved_scale
    grad_rows = (
        kept_grad.astype(jnp.float32)
        + saved_scale * weighted
        - saved_values * scale_cube * correction
    ).astype(jnp.bfloat16)
    section_edges = jnp.stack([grad_rows, forward_out], axis=0)
    padded = padded_2(section_edges, (("section", 0),), 1)
    down_part = contract_rows(back_rank, saved_normed)
    up_part = contract_rows(saved_act, kept_grad)
    down_sum, up_sum = in_one_piece(
        (down_part.astype(jnp.bfloat16), up_part.astype(jnp.bfloat16)), "dp", 0, 1
    )
    mean_weight = 1.0 / lax.axis_size("dp")
    grad_down = (down_sum * mean_weight).astype(jnp.bfloat16)
    grad_up = (up_sum * mean_weight).astype(jnp.bfloat16)
    return (padded[0][None, None], padded[3][None, None], grad_down[None], grad_up[None])


def solution(mesh):
    placed = (
        P("section", "dp", None, "tensor"),
        P("section", "dp", None, "tensor"),
        P("section", "dp", None, "tensor"),
        P("section", "dp", None),
        P("section", "tensor"),
        P("section", None, "tensor"),
        P("section", None, "tensor"),
    )
    return jax.shard_map(
        shards,
        mesh=mesh,
        in_specs=placed,
        out_specs=(
            P("section", "dp", None, "tensor"),
            P("section", "dp", None, "tensor"),
            P("section", "dp", "tensor"),
            P("section", "dp", "tensor"),
        ),
        check_vma=False,
    )
```

profile of v0, /device:TPU:49, one launch (start us, length us, event | category | flops | bytes accessed | tf_op | source)
XLA Modules:
  0.0 135.0 jit_solution(6442550528054221270)
XLA Ops:
  0.6 0.0 copy-start
  0.6 0.0 copy-start.2
  0.7 0.0 copy-start.8
  0.7 0.0 copy-start.7
  0.7 1.5 %fusion.13 = f32[192]{0:T(256)S(1)} fusion(bf16[1,1,192,2048]{3,2,1,0:T(8,128)(2,1)} %param.7), kind=kLoop, calls=%fused_computation.22 | loop fusion | flops 1179456 | bytes 787200 | tf_op jit(solution)/shard_map/reduce_sum | solution.py:104
  2.2 0.0 copy-start.1
  2.2 1.4 %fusion.6 = f32[192]{0:T(256)S(1)} fusion(bf16[1,1,192,2048]{3,2,1,0:T(8,128)(2,1)} %param.8), kind=kLoop, calls=%fused_computation.15 | loop fusion | flops 1179456 | bytes 787200 | tf_op jit(solution)/shard_map/reduce_sum | solution.py:105
  3.6 0.0 copy-done.8
  3.6 0.6 fusion.40
  4.2 0.0 copy-done.7
  4.2 8.5 %all-reduce = (f32[192]{0:T(256)S(1)}, f32[192]{0:T(256)S(1)}) all-reduce(f32[192]{0:T(256)S(1)} %fusion.6, f32[192]{0:T(256)S(1)} %fusion.13), channel_id=1, replica_groups=mesh['section'=32,'tensor'=4,'dp'=6] {'tensor'}, use_global_device_ids=true, to_apply=%region_3.0 | all-reduce | flops 384 | bytes 3072 | tf_op jit(solution)/shard_map/psum | solution.py:102
  12.7 0.0 copy-done
  12.7 0.0 copy-done.2
  12.7 0.5 convolution_convert_fusion.4
  13.2 0.0 copy-start.5
  13.2 0.0 copy-start.6
  13.2 0.0 copy-done.1
  13.2 0.5 convolution_convert_fusion.3
  13.7 1.3 fusion.36
  15.0 0.0 copy-done.5
  15.0 0.0 copy-done.6
  15.0 0.5 convolution_convert_fusion.2
  15.5 0.1 pad_maximum_fusion.1
  15.6 7.8 %all_to_all.15 = bf16[4,576,48]{1,2,0:T(8,128)(2,1)S(1)} all-to-all(bf16[4,576,48]{1,2,0:T(8,128)(2,1)S(1)} %bitcast.85), channel_id=1, replica_groups=mesh['section'=32,'tensor'=4,'dp'=6] {'tensor'}, dimensions={0} | all-to-all | bytes 442368 | tf_op jit(solution)/shard_map/all_to_all | solution.py:17
  23.5 0.1 multiply_convert_fusion.1
  23.6 0.1 pad_maximum_fusion.2
  23.7 7.8 %all_to_all.16 = bf16[4,576,48]{1,2,0:T(8,128)(2,1)S(1)} all-to-all(bf16[4,576,48]{1,2,0:T(8,128)(2,1)S(1)} %broadcast_in_dim.43), channel_id=1, replica_groups=mesh['section'=32,'tensor'=4,'dp'=6] {'tensor'}, dimensions={0} | all-to-all | bytes 442368 | tf_op jit(solution)/shard_map/all_to_all | solution.py:32
  31.5 0.1 fusion.39
  31.6 0.4 convolution_convert_fusion
  32.1 0.5 convolution_convert_fusion.1
  32.5 1.3 pad_maximum_fusion
  33.8 10.5 %all-to-all-start.2 = ((bf16[6,32,4096]{2,1,0:T(8,128)(2,1)}), bf16[6,32,4096]{2,1,0:T(8,128)(2,1)S(1)}, u32[]{:S(2)}, u32[]{:S(2)}) async-start(bf16[6,32,4096]{2,1,0:T(8,128)(2,1)} %bitcast.83), calls=%async_computation.2 | async-start | bytes 3145728 | tf_op jit(solution)/shard_map/all_to_all | solution.py:17
  44.3 2.6 %fusion.1 = bf16[1,192,2048]{2,1,0:T(8,128)(2,1)} fusion(bf16[192,192]{0,1:T(8,128)(2,1)S(1)} %bitcast.89, bf16[1,1,192,2048]{3,2,1,0:T(8,128)(2,1)} %param.7, bf16[1,192,2048]{2,1,0:T(8,128)(2,1)} %param.13), kind=kOutput, calls=%fused_computation.6 | convolution fusion | flops 152174592 | bytes 2433024 | tf_op jit(solution)/shard_map/dot_general | solution.py:141
  46.9 8.8 %collective-permute-start = (bf16[1,192,2048]{2,1,0:T(8,128)(2,1)}, bf16[1,192,2048]{2,1,0:T(8,128)(2,1)}, u32[]{:S(2)}, u32[]{:S(2)}) collective-permute-start(bf16[1,192,2048]{2,1,0:T(8,128)(2,1)} %fusion.1), channel_id=1, source_target_pairs={{0,24},{24,48},{48,72},{72,96},{96,120},{120,144},{144,168},{168,1... | collective-permute-start | bytes 2359304 | tf_op jit(solution)/shard_map/ppermute | solution.py:63
  55.8 1.5 %fusion.10 = (f32[192]{0:T(256)S(1)}, f32[192,2048]{1,0:T(8,128)}) fusion(bf16[1,1,192,2048]{3,2,1,0:T(8,128)(2,1)S(1)} %copy-done.1, bf16[192,192]{0,1:T(8,128)(2,1)S(1)} %bitcast.88, bf16[1,192,2048]{2,1,0:T(8,128)(2,1)S(1)} %copy-done, f32[2048]{0:T(1024)S(1)} %bitcast.94), kind=kOutput, calls=%fused_computation.19 | convolution fusion | flops 152567616 | bytes 3228416 | tf_op jit(solution)/shard_map/dot_general | solution.py:143
  57.3 6.8 %psum.23 = f32[192]{0:T(256)S(1)} all-reduce(f32[192]{0:T(256)S(1)} %get-tuple-element.18), channel_id=1, replica_groups=mesh['section'=32,'tensor'=4,'dp'=6] {'tensor'}, use_global_device_ids=true, to_apply=%region_6.7 | all-reduce | flops 192 | bytes 1536 | tf_op jit(solution)/shard_map/psum | solution.py:145
  64.2 2.1 %fusion.19 = bf16[1,192,2048]{2,1,0:T(8,128)(2,1)S(1)} fusion(bf16[1,1,192,2048]{3,2,1,0:T(8,128)(2,1)S(1)} %copy-done.1, f32[192,2048]{1,0:T(8,128)} %get-tuple-element.19, bf16[1,1,192,2048]{3,2,1,0:T(8,128)(2,1)} %param.9, f32[192]{0:T(256)S(1)} %broadcast_multiply_fusion, f32[192]{0:T(256)S(1)} %get-tuple-element.14, f32[192]{0:T(256)S(1)} %get-tuple-element.15, ...), kind=kLoop, calls=%fused_computation.31 | loop fusion | flops 3538944 | bytes 3934656 | tf_op jit(solution)/shard_map/stack | solution.py:152
  66.3 6.6 %collective-permute-start.1 = (bf16[1,192,2048]{2,1,0:T(8,128)(2,1)S(1)}, bf16[1,192,2048]{2,1,0:T(8,128)(2,1)S(1)}, u32[]{:S(2)}, u32[]{:S(2)}) collective-permute-start(bf16[1,192,2048]{2,1,0:T(8,128)(2,1)S(1)} %fusion.19), channel_id=1, source_target_pairs={{24,0},{48,24},{72,48},{96,72},{120,96},{144,120},{168,144},{192,1... | collective-permute-start | bytes 2359304 | tf_op jit(solution)/shard_map/ppermute | solution.py:65
  72.9 57.2 %collective-permute-done = bf16[1,192,2048]{2,1,0:T(8,128)(2,1)} collective-permute-done((bf16[1,192,2048]{2,1,0:T(8,128)(2,1)}, bf16[1,192,2048]{2,1,0:T(8,128)(2,1)}, u32[]{:S(2)}, u32[]{:S(2)}) %collective-permute-start) | collective-permute-done | bytes 786464 | tf_op jit(solution)/shard_map/ppermute | solution.py:63
  130.1 0.0 collective-permute-done.1
  130.2 0.0 copy-start.3
  130.2 0.9 copy-done.3
  131.0 0.0 all-to-all-done.2
  131.0 0.2 convert_reduce_fusion
  131.2 0.0 copy-start.4
  131.3 0.7 fusion.34
  132.0 2.1 %copy.13 = bf16[1,1,192,2048]{3,2,1,0:T(8,128)(2,1)} copy(bf16[1,1,192,2048]{3,2,1,0:T(8,128)(2,1)} %bitcast.15) | data formatting | bytes 1572864
  134.1 0.0 copy-done.4
  134.1 0.9 copy.14
  (5 shorter events, 0.1 us)
Async XLA Ops:
  0.6 12.1 %copy-start = (bf16[1,192,2048]{2,1,0:T(8,128)(2,1)S(1)}, bf16[1,192,2048]{2,1,0:T(8,128)(2,1)}, u32[]{:S(2)}) copy-start(bf16[1,192,2048]{2,1,0:T(8,128)(2,1)} %param.12) | copy-start | bytes 2359300
  0.6 12.1 %copy-start.2 = (bf16[1,1,192,2048]{3,2,1,0:T(8,128)(2,1)S(1)}, bf16[1,1,192,2048]{3,2,1,0:T(8,128)(2,1)}, u32[]{:S(2)}) copy-start(bf16[1,1,192,2048]{3,2,1,0:T(8,128)(2,1)} %param.7) | copy-start | bytes 2359300
  0.7 3.0 %copy-start.8 = (s32[1,1,2]{2,1,0:T(1,128)S(1)}, s32[1,1,2]{2,1,0:T(1,128)}, u32[]{:S(2)}) copy-start(s32[1,1,2]{2,1,0:T(1,128)} %param.10) | copy-start | bytes 28
  0.7 3.5 %copy-start.7 = (bf16[1,2048]{1,0:T(2,128)(2,1)S(1)}, bf16[1,2048]{1,0:T(2,128)(2,1)}, u32[]{:S(2)}) copy-start(bf16[1,2048]{1,0:T(2,128)(2,1)} %param.11) | copy-start | bytes 12292
  2.2 11.1 %copy-start.1 = (bf16[1,1,192,2048]{3,2,1,0:T(8,128)(2,1)S(1)}, bf16[1,1,192,2048]{3,2,1,0:T(8,128)(2,1)}, u32[]{:S(2)}) copy-start(bf16[1,1,192,2048]{3,2,1,0:T(8,128)(2,1)} %param.8) | copy-start | bytes 2359300
  13.2 1.8 %copy-start.5 = (bf16[1,192,2048]{2,1,0:T(8,128)(2,1)S(1)}, bf16[1,192,2048]{2,1,0:T(8,128)(2,1)}, u32[]{:S(2)}) copy-start(bf16[1,192,2048]{2,1,0:T(8,128)(2,1)} %param.13) | copy-start | bytes 2359300
  13.2 1.8 %copy-start.6 = (bf16[1,1,192,2048]{3,2,1,0:T(8,128)(2,1)S(1)}, bf16[1,1,192,2048]{3,2,1,0:T(8,128)(2,1)}, u32[]{:S(2)}) copy-start(bf16[1,1,192,2048]{3,2,1,0:T(8,128)(2,1)} %param.9) | copy-start | bytes 2359300
  33.8 97.2 %all-to-all-start.2 = ((bf16[6,32,4096]{2,1,0:T(8,128)(2,1)}), bf16[6,32,4096]{2,1,0:T(8,128)(2,1)S(1)}, u32[]{:S(2)}, u32[]{:S(2)}) async-start(bf16[6,32,4096]{2,1,0:T(8,128)(2,1)} %bitcast.83), calls=%async_computation.2 | async-start | bytes 3145728 | tf_op jit(solution)/shard_map/all_to_all | solution.py:17
  46.9 83.2 %collective-permute-start = (bf16[1,192,2048]{2,1,0:T(8,128)(2,1)}, bf16[1,192,2048]{2,1,0:T(8,128)(2,1)}, u32[]{:S(2)}, u32[]{:S(2)}) collective-permute-start(bf16[1,192,2048]{2,1,0:T(8,128)(2,1)} %fusion.1), channel_id=1, source_target_pairs={{0,24},{24,48},{48,72},{72,96},{96,120},{120,144},{144,168},{168,1... | collective-permute-start | bytes 2359304 | tf_op jit(solution)/shard_map/ppermute | solution.py:63
  66.3 63.9 %collective-permute-start.1 = (bf16[1,192,2048]{2,1,0:T(8,128)(2,1)S(1)}, bf16[1,192,2048]{2,1,0:T(8,128)(2,1)S(1)}, u32[]{:S(2)}, u32[]{:S(2)}) collective-permute-start(bf16[1,192,2048]{2,1,0:T(8,128)(2,1)S(1)} %fusion.19), channel_id=1, source_target_pairs={{24,0},{48,24},{72,48},{96,72},{120,96},{144,120},{168,144},{192,1... | collective-permute-start | bytes 2359304 | tf_op jit(solution)/shard_map/ppermute | solution.py:65
  130.2 0.9 copy-start.3
  131.2 2.8 %copy-start.4 = (bf16[1,192,2048]{2,1,0:T(8,128)(2,1)S(1)}, bf16[1,192,2048]{2,1,0:T(8,128)(2,1)}, u32[]{:S(2)}) copy-start(bf16[1,192,2048]{2,1,0:T(8,128)(2,1)} %copy-done.3) | copy-start | bytes 2359300
where the time goes:
time: 135 us
  waiting for transfers between devices  57.2 us (42%)
  blocking collectives  31 us (23%)
  starting transfers between devices  25.9 us (19%)
  other arithmetic  8.98 us (7%)
  matrix products  6.46 us (5%)
  local copies, waits for them, and re-layouts  4.59 us (3%)
    ppermute x1, waiting for transfers between devices, padded_2(): lax.ppermute(tail, axis, [(i, (i + 1) % count) for i in range(ends)])  57.2 us
    all_to_all x1, starting transfers between devices, summed_on_arrival(): lax.all_to_all(pieces, axis, split_axis=0, concat_axis=0, tiled=True)  10.5 us
    ppermute x1, starting transfers between devices, padded_2(): lax.ppermute(tail, axis, [(i, (i + 1) % count) for i in range(ends)])  8.82 us
    psum x1, blocking collectives, shards(): lax.psum((jnp.sum(forward_values * forward_values, axis=1), jnp.sum(saved...  8.48 us
    all_to_all x1, blocking collectives, summed_on_arrival(): lax.all_to_all(pieces, axis, split_axis=0, concat_axis=0, tiled=True)  7.82 us
    all_to_all x1, blocking collectives, sent_to_all(): return lax.all_to_all(copies, axis, split_axis=0, concat_axis=0, tiled=True)  7.82 us
    psum x1, blocking collectives, shards(): lax.psum(jnp.sum(saved_values * weighted, axis=1), 'tensor')[:, None]  6.85 us
    ppermute x1, starting transfers between devices, padded_2(): lax.ppermute(head, axis, [((i + 1) % count, i) for i in range(ends)])  6.64 us
  transfers between devices with their start and end apart: 3, of which 1 were waited for; matrix products, arithmetic and copies ran while one was open for 5% of the time, Pallas kernels for 0%

commit v1 on v0

v1 whole, which is shorter than its diff:
```python
import functools

import jax
import jax.numpy as jnp
from jax import lax
from jax.experimental import pallas as pl
from jax.experimental.pallas import tpu as pltpu
from jax.sharding import PartitionSpec as P

EPSILON = 1e-05
MESH = pl.DeviceIdType.MESH
CHUNKS = ((0, 16), (16, 32), (48, 64), (112, 80))
TILE = 256
ROW_BLOCK = 16


def remote(src, dst, send_sem, recv_sem, target):
    return pltpu.make_async_remote_copy(
        src_ref=src, dst_ref=dst, send_sem=send_sem, recv_sem=recv_sem, device_id=target, device_id_type=MESH
    )


def contract(left, right, dims):
    return lax.dot_general(left, right, ((dims[:1], dims[1:]), ((), ())), preferred_element_type=jnp.float32)


def kernel(
    n_section, n_tensor, n_dp,
    lens, gain, f_hbm, s_hbm, g_hbm, d_hbm, u_hbm,
    next_f, next_g, grad_down, grad_up,
    fwd, saved, kept, down, up, squares, fwd_out, back_out, own, others, sact_all, back_all,
    parts, from_core, chip_sum, from_chip, mean_out,
    load_sem, x_send, x_recv, f_send, f_recv, b_send, b_recv, c_send, c_recv, z_send, z_recv, out_sem,
):
    rows, cols = fwd.shape
    units = down.shape[0]
    width = cols * n_tensor
    sec, ten, dp = lax.axis_index("section"), lax.axis_index("tensor"), lax.axis_index("dp")
    n_z = n_dp // 2
    z, core = dp // 2, dp % 2
    has_next, has_prev = sec < n_section - 1, sec > 0

    loads = []
    for i, (src, dst) in enumerate(((d_hbm, down), (s_hbm, saved), (u_hbm, up), (g_hbm, kept), (f_hbm, fwd))):
        loads.append(pltpu.make_async_copy(src, dst, load_sem.at[i]))
        loads[-1].start()
    down_load, saved_load, up_load, kept_load, fwd_load = loads

    x_peers = [{"tensor": lax.rem(ten + k, n_tensor)} for k in range(1, n_tensor)]
    core_peer = {"dp": z * 2 + 1 - core}
    z_peers = [{"dp": lax.rem(z + k, n_z) * 2 + core} for k in range(1, n_z)]
    barrier = pltpu.get_barrier_semaphore()
    for peer in (*x_peers, core_peer, *z_peers):
        pl.semaphore_signal(barrier, inc=1, device_id=peer, device_id_type=MESH)

    @pl.when(has_next)
    def _():
        pl.semaphore_signal(barrier, inc=1, device_id={"section": sec + 1}, device_id_type=MESH)

    @pl.when(has_prev)
    def _():
        pl.semaphore_signal(barrier, inc=1, device_id={"section": sec - 1}, device_id_type=MESH)

    def row_blocks(body):
        def step(i, carry):
            body(pl.ds(pl.multiple_of(i * ROW_BLOCK, ROW_BLOCK), ROW_BLOCK))
            return carry

        lax.fori_loop(0, rows // ROW_BLOCK, step, 0, unroll=True)

    def col_tiles(body):
        def step(i, carry):
            body(pl.ds(pl.multiple_of(i * TILE, TILE), TILE))
            return carry

        lax.fori_loop(0, cols // TILE, step, 0, unroll=2)

    gain_row = gain[...].astype(jnp.float32)

    def scale_down(r):
        down[r, :] = (down[r, :].astype(jnp.float32) * gain_row).astype(jnp.bfloat16)

    def squares_of(ref):
        def body(r):
            values = ref[r, :].astype(jnp.float32)
            values = values * values
            total = values[:, :128]
            for j in range(1, cols // 128):
                total = total + values[:, j * 128 : (j + 1) * 128]
            squares[r, :] = total

        row_blocks(body)
        return jnp.sum(squares[...], axis=1, keepdims=True)

    def place(which, part, total):
        part = part.astype(jnp.bfloat16)
        for r0, n in CHUNKS:
            at = 3 * r0 + which * n
            own[at : at + n, :units] = part[r0 : r0 + n]
            if total is not None:
                own[at : at + n, units:] = jnp.broadcast_to(total[r0 : r0 + n].astype(jnp.bfloat16), (n, 256 - units))

    down_load.wait()
    row_blocks(scale_down)
    saved_load.wait()
    place(1, contract(saved[...], down[...], (1, 1)), squares_of(saved))

    kept_load.wait()

    def mask_rows(r):
        row = r.start + lax.broadcasted_iota(jnp.int32, (ROW_BLOCK, cols), 0)
        half = rows // 2
        second = row >= half
        position = jnp.where(second, row - half, row)
        limit = jnp.where(second, lens[1], lens[0])
        values = kept[r, :].astype(jnp.float32)
        kept[r, :] = jnp.where(position < limit, values, 0.0).astype(jnp.bfloat16)

    row_blocks(mask_rows)
    up_load.wait()
    place(2, contract(kept[...], up[...], (1, 1)), None)
    fwd_load.wait()
    place(0, contract(fwd[...], down[...], (1, 1)), squares_of(fwd))

    sections = (sec + n_section - 1) // n_section + (2 * n_section - 2 - sec) // n_section
    pl.semaphore_wait(barrier, n_tensor - 1 + 1 + n_z - 1 + sections)

    x_copies = []
    for c, (r0, n) in enumerate(CHUNKS):
        at = pl.ds(3 * r0, 3 * n)
        x_copies.append([
            remote(own.at[at], others.at[k, at], x_send.at[c, k], x_recv.at[c, k], x_peers[k])
            for k in range(n_tensor - 1)
        ])
        for copy in x_copies[-1]:
            copy.start()

    f_copies, b_copies = [], []
    for c, (r0, n) in enumerate(CHUNKS):
        for copy in x_copies[c]:
            copy.wait_recv()

        def summed(which):
            at = pl.ds(3 * r0 + which * n, n)
            total = own[at, :].astype(jnp.float32)
            for k in range(n_tensor - 1):
                total = total + others[k, at, :].astype(jnp.float32)
            return total

        r = pl.ds(r0, n)
        saved_total = summed(1)
        saved_scale = lax.rsqrt(saved_total[:, units : units + 1] / width + EPSILON)
        saved_rank = saved_total[:, :units] * saved_scale
        gate = jax.nn.sigmoid(saved_rank)
        sact_all[r, :] = (saved_rank * gate).astype(jnp.bfloat16)
        back = summed(2)[:, :units] * (gate * (1.0 + saved_rank * (1.0 - gate)))
        pull = saved_scale * saved_scale * (jnp.sum(back * saved_rank, axis=1, keepdims=True) / width)
        back = (back * saved_scale).astype(jnp.bfloat16)
        back_all[r, :] = back
        fwd_total = summed(0)
        fwd_scale = lax.rsqrt(fwd_total[:, units : units + 1] / width + EPSILON)
        act = jax.nn.silu(fwd_total[:, :units] * fwd_scale).astype(jnp.bfloat16)

        def back_tile(t):
            weighted = contract(back, down[:, t], (1, 0))
            values = kept[r, t].astype(jnp.float32) + weighted - saved[r, t].astype(jnp.float32) * pull
            back_out[r, t] = values.astype(jnp.bfloat16)

        col_tiles(back_tile)
        b_copies.append(remote(back_out.at[r], next_g.at[r], b_send.at[c], b_recv.at[c], {"section": sec - 1}))

        @pl.when(has_prev)
        def _():
            b_copies[c].start()

        def fwd_tile(t):
            raised = contract(act, up[:, t], (1, 0))
            fwd_out[r, t] = (fwd[r, t].astype(jnp.float32) + raised).astype(jnp.bfloat16)

        col_tiles(fwd_tile)
        f_copies.append(remote(fwd_out.at[r], next_f.at[r], f_send.at[c], f_recv.at[c], {"section": sec + 1}))

        @pl.when(has_next)
        def _():
            f_copies[c].start()

    def part_tile(t):
        share = units // n_dp
        down_part = (contract(back_all[...], saved[:, t], (0, 0)) * gain[:, t].astype(jnp.float32)).astype(jnp.bfloat16)
        up_part = contract(sact_all[...], kept[:, t], (0, 0)).astype(jnp.bfloat16)
        for i in range(n_dp):
            at = slice(i * share, (i + 1) * share)
            parts[i % 2, i // 2, 0, :, t] = down_part[at]
            parts[i % 2, i // 2, 1, :, t] = up_part[at]

    col_tiles(part_tile)
    order = [lax.rem(z + k, n_z) for k in (*range(1, n_z), 0)]
    c_copies = []
    for i, at in enumerate(order):
        c_copies.append(remote(parts.at[1 - core, at], from_core.at[i], c_send.at[i], c_recv.at[i], core_peer))
        c_copies[-1].start()
    z_copies = []
    for i, at in enumerate(order):
        c_copies[i].wait_recv()

        def add(t):
            for a in range(2):
                chip_sum[i, a, :, t] = (
                    parts[core, at, a, :, t].astype(jnp.float32) + from_core[i, a, :, t].astype(jnp.float32)
                ).astype(jnp.bfloat16)

        col_tiles(add)
        if i < n_z - 1:
            z_copies.append(remote(chip_sum.at[i], from_chip.at[i], z_send.at[i], z_recv.at[i], z_peers[i]))
            z_copies[-1].start()
    for copy in z_copies:
        copy.wait_recv()

    def finish(t):
        for a in range(2):
            total = chip_sum[n_z - 1, a, :, t].astype(jnp.float32)
            for i in range(n_z - 1):
                total = total + from_chip[i, a, :, t].astype(jnp.float32)
            mean_out[a, :, t] = (total * (1.0 / n_dp)).astype(jnp.bfloat16)

    col_tiles(finish)
    outs = [
        pltpu.make_async_copy(mean_out.at[a], dst, out_sem.at[a]) for a, dst in enumerate((grad_down, grad_up))
    ]
    for copy in outs:
        copy.start()

    for copies in x_copies:
        for copy in copies:
            copy.wait_send()
    for copy in (*c_copies, *z_copies):
        copy.wait_send()
    for c in range(len(CHUNKS)):
        @pl.when(has_prev)
        def _():
            b_copies[c].wait_send()
            f_copies[c].wait_recv()

        @pl.when(has_next)
        def _():
            f_copies[c].wait_send()
            b_copies[c].wait_recv()
    for copy in outs:
        copy.wait()


def solution(mesh):
    n_section, n_tensor, n_dp = (mesh.shape[a] for a in ("section", "tensor", "dp"))
    n_z = n_dp // 2

    def shards(forward_rows, saved_rows, output_grad, lengths, norm_gain, down_map, up_map):
        rows, cols = forward_rows.shape[2:]
        units = down_map.shape[1]
        share = units // n_dp
        n = len(CHUNKS)
        bf16 = jnp.bfloat16
        anywhere = pl.BlockSpec(memory_space=pl.ANY)
        dma = pltpu.SemaphoreType.DMA
        got_f, got_g, grad_down, grad_up = pl.pallas_call(
            functools.partial(kernel, n_section, n_tensor, n_dp),
            out_shape=(
                jax.ShapeDtypeStruct((rows, cols), bf16),
                jax.ShapeDtypeStruct((rows, cols), bf16),
                jax.ShapeDtypeStruct((share, cols), bf16),
                jax.ShapeDtypeStruct((share, cols), bf16),
            ),
            in_specs=[
                pl.BlockSpec(memory_space=pltpu.SMEM),
                pl.BlockSpec(memory_space=pltpu.VMEM),
                *[anywhere] * 5,
            ],
            out_specs=(anywhere,) * 4,
            scratch_shapes=[
                *[pltpu.VMEM((rows, cols), bf16)] * 3,
                *[pltpu.VMEM((units, cols), bf16)] * 2,
                pltpu.VMEM((rows, 128), jnp.float32),
                *[pltpu.VMEM((rows, cols), bf16)] * 2,
                pltpu.VMEM((3 * rows, 256), bf16),
                pltpu.VMEM((n_tensor - 1, 3 * rows, 256), bf16),
                *[pltpu.VMEM((rows, units), bf16)] * 2,
                pltpu.VMEM((2, n_z, 2, share, cols), bf16),
                pltpu.VMEM((n_z, 2, share, cols), bf16),
                pltpu.VMEM((n_z, 2, share, cols), bf16),
                pltpu.VMEM((n_z - 1, 2, share, cols), bf16),
                pltpu.VMEM((2, share, cols), bf16),
                dma((5,)),
                *[dma((n, n_tensor - 1))] * 2,
                *[dma((n,))] * 4,
                *[dma((n_z,))] * 2,
                *[dma((n_z - 1,))] * 2,
                dma((2,)),
            ],
            compiler_params=pltpu.CompilerParams(
                collective_id=0, has_side_effects=True, vmem_limit_bytes=48 * 1024 * 1024
            ),
        )(
            lengths[0, 0],
            norm_gain,
            forward_rows[0, 0],
            saved_rows[0, 0],
            output_grad[0, 0],
            down_map[0],
            up_map[0],
        )
        sec = lax.axis_index("section")
        next_inputs = jnp.where(sec > 0, got_f, jnp.zeros_like(got_f))
        next_grads = jnp.where(sec < n_section - 1, got_g, jnp.zeros_like(got_g))
        return next_inputs[None, None], next_grads[None, None], grad_down[None], grad_up[None]

    wide = P("section", "dp", None, "tensor")
    return jax.shard_map(
        shards,
        mesh=mesh,
        in_specs=(
            wide, wide, wide, P("section", "dp", None), P("section", "tensor"),
            P("section", None, "tensor"), P("section", None, "tensor"),
        ),
        out_specs=(wide, wide, P("section", "dp", "tensor"), P("section", "dp", "tensor")),
        check_vma=False,
    )
```

time: 135 us -> 94.3 us (0.70)
  the two profiles are of different devices: /device:TPU:49 before, /device:TPU:40 now
where the time goes in v1:
time: 94.3 us; the launch traced here: 93.9 us
  Pallas kernels  84.3 us (89%)
  local copies, waits for them, and re-layouts  7.65 us (8%)
  other arithmetic  1.25 us (1%)
    pallas_call x1, Pallas kernels, shards(): pl.pallas_call(functools.partial(kernel, n_section, n_tensor, n_dp), out_...  84.3 us
    unnamed x16, local copies, waits for them, and re-layouts  7.65 us

profile of v1, /device:TPU:40, one launch (start us, length us, event | category | flops | bytes accessed | tf_op | source)
XLA Modules:
  0.0 93.9 jit_solution(11111387009774282723)
XLA Ops:
  0.6 0.0 copy-start.5
  0.7 0.0 copy-start.6
  0.7 0.7 copy-done.5
  1.3 0.0 copy-done.6
  1.3 0.0 copy-start
  1.3 1.1 %copy-done = bf16[1,1,192,2048]{3,2,1,0:T(8,128)(2,1)S(1)} copy-done((bf16[1,1,192,2048]{3,2,1,0:T(8,128)(2,1)S(1)}, bf16[1,1,192,2048]{3,2,1,0:T(8,128)(2,1)}, u32[]{:S(2)}) %copy-start) | copy-done | bytes 786456
  2.5 0.0 copy-start.1
  2.5 1.1 %copy-done.1 = bf16[1,1,192,2048]{3,2,1,0:T(8,128)(2,1)S(1)} copy-done((bf16[1,1,192,2048]{3,2,1,0:T(8,128)(2,1)S(1)}, bf16[1,1,192,2048]{3,2,1,0:T(8,128)(2,1)}, u32[]{:S(2)}) %copy-start.1) | copy-done | bytes 786456
  3.6 0.0 copy-start.2
  3.6 1.1 %copy-done.2 = bf16[1,1,192,2048]{3,2,1,0:T(8,128)(2,1)S(1)} copy-done((bf16[1,1,192,2048]{3,2,1,0:T(8,128)(2,1)S(1)}, bf16[1,1,192,2048]{3,2,1,0:T(8,128)(2,1)}, u32[]{:S(2)}) %copy-start.2) | copy-done | bytes 786456
  4.7 0.0 copy-start.3
  4.7 1.1 %copy-done.3 = bf16[1,192,2048]{2,1,0:T(8,128)(2,1)S(1)} copy-done((bf16[1,192,2048]{2,1,0:T(8,128)(2,1)S(1)}, bf16[1,192,2048]{2,1,0:T(8,128)(2,1)}, u32[]{:S(2)}) %copy-start.3) | copy-done | bytes 786456
  5.9 0.0 copy-start.4
  5.9 1.1 %copy-done.4 = bf16[1,192,2048]{2,1,0:T(8,128)(2,1)S(1)} copy-done((bf16[1,192,2048]{2,1,0:T(8,128)(2,1)S(1)}, bf16[1,192,2048]{2,1,0:T(8,128)(2,1)}, u32[]{:S(2)}) %copy-start.4) | copy-done | bytes 786456
  7.0 84.3 %shard_map.102 = (bf16[192,2048]{1,0:T(8,128)(2,1)S(1)}, bf16[192,2048]{1,0:T(8,128)(2,1)S(1)}, bf16[32,2048]{1,0:T(8,128)(2,1)S(1)}, bf16[32,2048]{1,0:T(8,128)(2,1)S(1)}) custom-call(s32[2]{0:T(128)S(1)} %bitcast.19, bf16[1,2048]{1,0:T(2,128)(2,1)S(1)} %copy-done.5, bf16[192,2048]{1,0:T(8,128)(2,1)S(1)} %bitcast.12, bf16[192,2048]{1,0:T(8,128)(2,1)S(1)} %bitcast.13, ...), custom_call_target="tpu_custom_call" | custom-call | tf_op jit(solution)/shard_map/pallas_call | solution.py:264
  91.3 1.2 %select_bitcast_fusion = (bf16[1,1,192,2048]{3,2,1,0:T(8,128)(2,1)}, bf16[1,1,192,2048]{3,2,1,0:T(8,128)(2,1)}) fusion(bf16[192,2048]{1,0:T(8,128)(2,1)S(1)} %get-tuple-element.9, pred[]{:T(512)S(6)} %lt.3, bf16[192,2048]{1,0:T(8,128)(2,1)S(1)} %get-tuple-element.8, pred[]{:T(512)S(6)} %gt.3), kind=kLoop, calls=%fused_computation | loop fusion | flops 786432 | bytes 3145730 | tf_op jit(solution)/shard_map/broadcast_in_dim | solution.py:313
  92.6 0.7 copy.13
  93.2 0.7 copy.14
Async XLA Ops:
  0.6 0.7 copy-start.5
  0.7 0.7 copy-start.6
  1.3 1.1 %copy-start = (bf16[1,1,192,2048]{3,2,1,0:T(8,128)(2,1)S(1)}, bf16[1,1,192,2048]{3,2,1,0:T(8,128)(2,1)}, u32[]{:S(2)}) copy-start(bf16[1,1,192,2048]{3,2,1,0:T(8,128)(2,1)} %param.7) | copy-start | bytes 2359300
  2.5 1.1 %copy-start.1 = (bf16[1,1,192,2048]{3,2,1,0:T(8,128)(2,1)S(1)}, bf16[1,1,192,2048]{3,2,1,0:T(8,128)(2,1)}, u32[]{:S(2)}) copy-start(bf16[1,1,192,2048]{3,2,1,0:T(8,128)(2,1)} %param.8) | copy-start | bytes 2359300
  3.6 1.1 %copy-start.2 = (bf16[1,1,192,2048]{3,2,1,0:T(8,128)(2,1)S(1)}, bf16[1,1,192,2048]{3,2,1,0:T(8,128)(2,1)}, u32[]{:S(2)}) copy-start(bf16[1,1,192,2048]{3,2,1,0:T(8,128)(2,1)} %param.9) | copy-start | bytes 2359300
  4.7 1.1 %copy-start.3 = (bf16[1,192,2048]{2,1,0:T(8,128)(2,1)S(1)}, bf16[1,192,2048]{2,1,0:T(8,128)(2,1)}, u32[]{:S(2)}) copy-start(bf16[1,192,2048]{2,1,0:T(8,128)(2,1)} %param.12) | copy-start | bytes 2359300
  5.9 1.1 %copy-start.4 = (bf16[1,192,2048]{2,1,0:T(8,128)(2,1)S(1)}, bf16[1,192,2048]{2,1,0:T(8,128)(2,1)}, u32[]{:S(2)}) copy-start(bf16[1,192,2048]{2,1,0:T(8,128)(2,1)} %param.13) | copy-start | bytes 2359300

commit v2 on v1

--- a/solution.py
+++ b/solution.py
@@ -12,6 +12,7 @@
 CHUNKS = ((0, 16), (16, 32), (48, 64), (112, 80))
 TILE = 256
 ROW_BLOCK = 16
+PIECES = 4
 
 
 def remote(src, dst, send_sem, recv_sem, target):
@@ -26,11 +27,11 @@
 
 def kernel(
     n_section, n_tensor, n_dp,
-    lens, gain, f_hbm, s_hbm, g_hbm, d_hbm, u_hbm,
+    lens_hbm, gain_hbm, f_hbm, s_hbm, g_hbm, d_hbm, u_hbm,
     next_f, next_g, grad_down, grad_up,
     fwd, saved, kept, down, up, squares, fwd_out, back_out, own, others, sact_all, back_all,
-    parts, from_core, chip_sum, from_chip, mean_out,
-    load_sem, x_send, x_recv, f_send, f_recv, b_send, b_recv, c_send, c_recv, z_send, z_recv, out_sem,
+    parts, from_core, chip_sum, from_chip,
+    lens, gain, small_sem, load_sem, x_send, x_recv, f_send, f_recv, b_send, b_recv, c_send, c_recv, z_send, z_recv,
 ):
     rows, cols = fwd.shape
     units = down.shape[0]
@@ -40,11 +41,22 @@
     z, core = dp // 2, dp % 2
     has_next, has_prev = sec < n_section - 1, sec > 0
 
+    lens_load = pltpu.make_async_copy(lens_hbm, lens, small_sem.at[0])
+    gain_load = pltpu.make_async_copy(gain_hbm, gain, small_sem.at[1])
+    gain_load.start()
+    lens_load.start()
     loads = []
     for i, (src, dst) in enumerate(((d_hbm, down), (s_hbm, saved), (u_hbm, up), (g_hbm, kept), (f_hbm, fwd))):
-        loads.append(pltpu.make_async_copy(src, dst, load_sem.at[i]))
-        loads[-1].start()
+        loads.append([])
+        for j in range(PIECES):
+            at = pl.ds(j * (rows // PIECES), rows // PIECES)
+            loads[-1].append(pltpu.make_async_copy(src.at[at], dst.at[at], load_sem.at[i, j]))
+            loads[-1][-1].start()
     down_load, saved_load, up_load, kept_load, fwd_load = loads
+
+    def loaded(pieces):
+        for piece in pieces:
+            piece.wait()
 
     x_peers = [{"tensor": lax.rem(ten + k, n_tensor)} for k in range(1, n_tensor)]
     core_peer = {"dp": z * 2 + 1 - core}
@@ -75,6 +87,7 @@
 
         lax.fori_loop(0, cols // TILE, step, 0, unroll=2)
 
+    gain_load.wait()
     gain_row = gain[...].astype(jnp.float32)
 
     def scale_down(r):
@@ -100,12 +113,13 @@
             if total is not None:
                 own[at : at + n, units:] = jnp.broadcast_to(total[r0 : r0 + n].astype(jnp.bfloat16), (n, 256 - units))
 
-    down_load.wait()
+    loaded(down_load)
     row_blocks(scale_down)
-    saved_load.wait()
+    loaded(saved_load)
     place(1, contract(saved[...], down[...], (1, 1)), squares_of(saved))
 
-    kept_load.wait()
+    loaded(kept_load)
+    lens_load.wait()
 
     def mask_rows(r):
         row = r.start + lax.broadcasted_iota(jnp.int32, (ROW_BLOCK, cols), 0)
@@ -117,13 +131,21 @@
         kept[r, :] = jnp.where(position < limit, values, 0.0).astype(jnp.bfloat16)
 
     row_blocks(mask_rows)
-    up_load.wait()
+    loaded(up_load)
     place(2, contract(kept[...], up[...], (1, 1)), None)
-    fwd_load.wait()
+    loaded(fwd_load)
     place(0, contract(fwd[...], down[...], (1, 1)), squares_of(fwd))
 
     sections = (sec + n_section - 1) // n_section + (2 * n_section - 2 - sec) // n_section
     pl.semaphore_wait(barrier, n_tensor - 1 + 1 + n_z - 1 + sections)
+
+    @pl.when(sec == 0)
+    def _():
+        next_f[...] = jnp.zeros_like(next_f)
+
+    @pl.when(sec == n_section - 1)
+    def _():
+        next_g[...] = jnp.zeros_like(next_g)
 
     x_copies = []
     for c, (r0, n) in enumerate(CHUNKS):
@@ -221,14 +243,9 @@
             total = chip_sum[n_z - 1, a, :, t].astype(jnp.float32)
             for i in range(n_z - 1):
                 total = total + from_chip[i, a, :, t].astype(jnp.float32)
-            mean_out[a, :, t] = (total * (1.0 / n_dp)).astype(jnp.bfloat16)
+            (grad_down, grad_up)[a][:, t] = (total * (1.0 / n_dp)).astype(jnp.bfloat16)
 
     col_tiles(finish)
-    outs = [
-        pltpu.make_async_copy(mean_out.at[a], dst, out_sem.at[a]) for a, dst in enumerate((grad_down, grad_up))
-    ]
-    for copy in outs:
-        copy.start()
 
     for copies in x_copies:
         for copy in copies:
@@ -245,7 +262,18 @@
         def _():
             f_copies[c].wait_send()
             b_copies[c].wait_recv()
-    for copy in outs:
+
+
+def put_out(*refs):
+    sources, targets, sem = refs[:4], refs[4:8], refs[8]
+    copies = []
+    for i in range(4):
+        n = sources[i].shape[0] // PIECES
+        for j in range(PIECES):
+            at = pl.ds(j * n, n)
+            copies.append(pltpu.make_async_copy(sources[i].at[at], targets[i].at[at], sem.at[i, j]))
+            copies[-1].start()
+    for copy in copies:
         copy.wait()
 
 
@@ -259,9 +287,10 @@
         share = units // n_dp
         n = len(CHUNKS)
         bf16 = jnp.bfloat16
-        anywhere = pl.BlockSpec(memory_space=pl.ANY)
+        in_hbm = pl.BlockSpec(memory_space=pltpu.HBM)
+        in_vmem = pl.BlockSpec(memory_space=pltpu.VMEM)
         dma = pltpu.SemaphoreType.DMA
-        got_f, got_g, grad_down, grad_up = pl.pallas_call(
+        results = pl.pallas_call(
             functools.partial(kernel, n_section, n_tensor, n_dp),
             out_shape=(
                 jax.ShapeDtypeStruct((rows, cols), bf16),
@@ -270,11 +299,9 @@
                 jax.ShapeDtypeStruct((share, cols), bf16),
             ),
             in_specs=[
-                pl.BlockSpec(memory_space=pltpu.SMEM),
-                pl.BlockSpec(memory_space=pltpu.VMEM),
-                *[anywhere] * 5,
+                *[in_hbm] * 7,
             ],
-            out_specs=(anywhere,) * 4,
+            out_specs=(in_vmem,) * 4,
             scratch_shapes=[
                 *[pltpu.VMEM((rows, cols), bf16)] * 3,
                 *[pltpu.VMEM((units, cols), bf16)] * 2,
@@ -287,30 +314,35 @@
                 pltpu.VMEM((n_z, 2, share, cols), bf16),
                 pltpu.VMEM((n_z, 2, share, cols), bf16),
                 pltpu.VMEM((n_z - 1, 2, share, cols), bf16),
-                pltpu.VMEM((2, share, cols), bf16),
-                dma((5,)),
+                pltpu.SMEM((2,), jnp.int32),
+                pltpu.VMEM((1, cols), bf16),
+                dma((2,)),
+                dma((5, PIECES)),
                 *[dma((n, n_tensor - 1))] * 2,
                 *[dma((n,))] * 4,
                 *[dma((n_z,))] * 2,
                 *[dma((n_z - 1,))] * 2,
-                dma((2,)),
             ],
             compiler_params=pltpu.CompilerParams(
                 collective_id=0, has_side_effects=True, vmem_limit_bytes=48 * 1024 * 1024
             ),
         )(
-            lengths[0, 0],
-            norm_gain,
-            forward_rows[0, 0],
-            saved_rows[0, 0],
-            output_grad[0, 0],
-            down_map[0],
-            up_map[0],
+            *(
+                pltpu.with_memory_space_constraint(a, pltpu.HBM)
+                for a in (
+                    lengths[0, 0], norm_gain, forward_rows[0, 0], saved_rows[0, 0], output_grad[0, 0], down_map[0],
+                    up_map[0],
+                )
+            )
         )
-        sec = lax.axis_index("section")
-        next_inputs = jnp.where(sec > 0, got_f, jnp.zeros_like(got_f))
-        next_grads = jnp.where(sec < n_section - 1, got_g, jnp.zeros_like(got_g))
-        return next_inputs[None, None], next_grads[None, None], grad_down[None], grad_up[None]
+        got_f, got_g, grad_down, grad_up = pl.pallas_call(
+            put_out,
+            out_shape=tuple(jax.ShapeDtypeStruct(a.shape, a.dtype) for a in results),
+            in_specs=[pl.BlockSpec(memory_space=pl.ANY)] * 4,
+            out_specs=(in_hbm,) * 4,
+            scratch_shapes=[dma((4, PIECES))],
+        )(*(pltpu.with_memory_space_constraint(a, pltpu.VMEM) for a in results))
+        return got_f[None, None], got_g[None, None], grad_down[None], grad_up[None]
 
     wide = P("section", "dp", None, "tensor")
     return jax.shard_map(

time: 94.3 us -> 85.5 us (0.907)
  the two profiles are of different devices: /device:TPU:40 before, /device:TPU:49 now
where the time goes in v2:
time: 85.5 us; the launch traced here: 84.6 us
  Pallas kernels  84 us (98%)
    pallas_call x1, Pallas kernels, shards(): pl.pallas_call(functools.partial(kernel, n_section, n_tensor, n_dp), out_...  82.6 us

profile of v2, /device:TPU:49, one launch (start us, length us, event | category | flops | bytes accessed | tf_op | source)
XLA Modules:
  0.0 84.6 jit_solution(6346346565940313585)
XLA Ops:
  0.6 82.6 %shard_map.102 = (bf16[192,2048]{1,0:T(8,128)(2,1)S(1)}, bf16[192,2048]{1,0:T(8,128)(2,1)S(1)}, bf16[32,2048]{1,0:T(8,128)(2,1)S(1)}, bf16[32,2048]{1,0:T(8,128)(2,1)S(1)}) custom-call(s32[2]{0:T(128)} %bitcast.15, bf16[1,2048]{1,0:T(2,128)(2,1)} %gain_hbm.1, bf16[192,2048]{1,0:T(8,128)(2,1)} %bitcast.10, bf16[192,2048]{1,0:T(8,128)(2,1)} %bitcast.11, ...), custom_call_target="tpu_custom_call" | custom-call | tf_op jit(solution)/shard_map/pallas_call | solution.py:293
  83.3 1.3 %shard_map.103 = (bf16[192,2048]{1,0:T(8,128)(2,1)}, bf16[192,2048]{1,0:T(8,128)(2,1)}, bf16[32,2048]{1,0:T(8,128)(2,1)}, bf16[32,2048]{1,0:T(8,128)(2,1)}) custom-call(bf16[192,2048]{1,0:T(8,128)(2,1)S(1)} %get-tuple-element.12.refs_0_, bf16[192,2048]{1,0:T(8,128)(2,1)S(1)} %get-tuple-element.13.refs_1_, bf16[32,2048]{1,0:T(8,128)(2,1)S(1)} %get-tuple-element.14.refs_2_, ...), custom_call_target="tpu_custom_call" | custom-call | tf_op jit(solution)/shard_map/pallas_call | solution.py:338

commit v3 on v2

--- a/solution.py
+++ b/solution.py
@@ -13,6 +13,8 @@
 TILE = 256
 ROW_BLOCK = 16
 PIECES = 4
+EARLY_EVERY = 4
+HEAD = CHUNKS[0][1]
 
 
 def remote(src, dst, send_sem, recv_sem, target):
@@ -31,7 +33,7 @@
     next_f, next_g, grad_down, grad_up,
     fwd, saved, kept, down, up, squares, fwd_out, back_out, own, others, sact_all, back_all,
     parts, from_core, chip_sum, from_chip,
-    lens, gain, small_sem, load_sem, x_send, x_recv, f_send, f_recv, b_send, b_recv, c_send, c_recv, z_send, z_recv,
+    lens, gain, near, far, small_sem, load_sem, x_send, x_recv, f_send, f_recv, b_send, b_recv, c_send, c_recv, z_send, z_recv,
 ):
     rows, cols = fwd.shape
     units = down.shape[0]
@@ -39,20 +41,30 @@
     sec, ten, dp = lax.axis_index("section"), lax.axis_index("tensor"), lax.axis_index("dp")
     n_z = n_dp // 2
     z, core = dp // 2, dp % 2
+    early = jnp.logical_and(lax.rem(sec, EARLY_EVERY) == 0, sec > 0)
     has_next, has_prev = sec < n_section - 1, sec > 0
 
     lens_load = pltpu.make_async_copy(lens_hbm, lens, small_sem.at[0])
     gain_load = pltpu.make_async_copy(gain_hbm, gain, small_sem.at[1])
-    gain_load.start()
-    lens_load.start()
-    loads = []
-    for i, (src, dst) in enumerate(((d_hbm, down), (s_hbm, saved), (u_hbm, up), (g_hbm, kept), (f_hbm, fwd))):
-        loads.append([])
-        for j in range(PIECES):
-            at = pl.ds(j * (rows // PIECES), rows // PIECES)
-            loads[-1].append(pltpu.make_async_copy(src.at[at], dst.at[at], load_sem.at[i, j]))
-            loads[-1][-1].start()
-    down_load, saved_load, up_load, kept_load, fwd_load = loads
+
+    def pieces_of(i, src, dst, bounds):
+        return [
+            pltpu.make_async_copy(src.at[pl.ds(lo, hi - lo)], dst.at[pl.ds(lo, hi - lo)], load_sem.at[i, j])
+            for j, (lo, hi) in enumerate(zip(bounds, bounds[1:]))
+        ]
+
+    quarters = tuple(range(0, units + 1, units // PIECES))
+    row_bounds = (0, HEAD, rows // 2, rows)
+    down_load = pieces_of(0, d_hbm, down, quarters)
+    up_load = pieces_of(1, u_hbm, up, quarters)
+    saved_load = pieces_of(2, s_hbm, saved, row_bounds)
+    fwd_load = pieces_of(3, f_hbm, fwd, row_bounds)
+    kept_load = pieces_of(4, g_hbm, kept, row_bounds)
+    for copy in (
+        gain_load, *down_load, saved_load[0], fwd_load[0], lens_load, kept_load[0], *up_load,
+        *saved_load[1:], *fwd_load[1:], *kept_load[1:],
+    ):
+        copy.start()
 
     def loaded(pieces):
         for piece in pieces:
@@ -62,38 +74,63 @@
     core_peer = {"dp": z * 2 + 1 - core}
     z_peers = [{"dp": lax.rem(z + k, n_z) * 2 + core} for k in range(1, n_z)]
     barrier = pltpu.get_barrier_semaphore()
-    for peer in (*x_peers, core_peer, *z_peers):
+
+    def enter(peer):
         pl.semaphore_signal(barrier, inc=1, device_id=peer, device_id_type=MESH)
 
+    for k in range(1, n_tensor):
+        enter({"tensor": lax.rem(ten + k, n_tensor), "dp": z * 2})
+    for k in range(1, n_z):
+        enter({"dp": lax.rem(z + k, n_z) * 2})
+
+    @pl.when(core == 1)
+    def _():
+        enter({"dp": z * 2})
+
     @pl.when(has_next)
     def _():
-        pl.semaphore_signal(barrier, inc=1, device_id={"section": sec + 1}, device_id_type=MESH)
+        enter({"section": sec + 1, "dp": z * 2 + 1})
 
     @pl.when(has_prev)
     def _():
-        pl.semaphore_signal(barrier, inc=1, device_id={"section": sec - 1}, device_id_type=MESH)
-
-    def row_blocks(body):
+        enter({"section": sec - 1, "dp": z * 2 + 1})
+
+    def meet_near():
+        @pl.when(core == 0)
+        def _():
+            pl.semaphore_wait(barrier, 2 * (n_tensor - 1) + 2 * (n_z - 1) + 1)
+            pl.semaphore_signal(near, inc=1, device_id=core_peer, device_id_type=MESH)
+
+        @pl.when(core == 1)
+        def _():
+            pl.semaphore_wait(near, 1)
+
+    def meet_sections():
+        @pl.when(core == 1)
+        def _():
+            sections = (sec + n_section - 1) // n_section + (2 * n_section - 2 - sec) // n_section
+            pl.semaphore_wait(barrier, 2 * sections)
+            pl.semaphore_signal(far, inc=1, device_id=core_peer, device_id_type=MESH)
+
+        @pl.when(core == 0)
+        def _():
+            pl.semaphore_wait(far, 1)
+
+    def row_blocks(body, lo, hi):
         def step(i, carry):
             body(pl.ds(pl.multiple_of(i * ROW_BLOCK, ROW_BLOCK), ROW_BLOCK))
             return carry
 
-        lax.fori_loop(0, rows // ROW_BLOCK, step, 0, unroll=True)
-
-    def col_tiles(body):
+        lax.fori_loop(lo // ROW_BLOCK, hi // ROW_BLOCK, step, 0, unroll=True)
+
+    def col_tiles(body, unroll=2):
         def step(i, carry):
             body(pl.ds(pl.multiple_of(i * TILE, TILE), TILE))
             return carry
 
-        lax.fori_loop(0, cols // TILE, step, 0, unroll=2)
-
-    gain_load.wait()
-    gain_row = gain[...].astype(jnp.float32)
-
-    def scale_down(r):
-        down[r, :] = (down[r, :].astype(jnp.float32) * gain_row).astype(jnp.bfloat16)
-
-    def squares_of(ref):
+        lax.fori_loop(0, cols // TILE, step, 0, unroll=unroll)
+
+    def squares_of(ref, lo, hi):
         def body(r):
             values = ref[r, :].astype(jnp.float32)
             values = values * values
@@ -102,24 +139,8 @@
                 total = total + values[:, j * 128 : (j + 1) * 128]
             squares[r, :] = total
 
-        row_blocks(body)
-        return jnp.sum(squares[...], axis=1, keepdims=True)
-
-    def place(which, part, total):
-        part = part.astype(jnp.bfloat16)
-        for r0, n in CHUNKS:
-            at = 3 * r0 + which * n
-            own[at : at + n, :units] = part[r0 : r0 + n]
-            if total is not None:
-                own[at : at + n, units:] = jnp.broadcast_to(total[r0 : r0 + n].astype(jnp.bfloat16), (n, 256 - units))
-
-    loaded(down_load)
-    row_blocks(scale_down)
-    loaded(saved_load)
-    place(1, contract(saved[...], down[...], (1, 1)), squares_of(saved))
-
-    loaded(kept_load)
-    lens_load.wait()
+        row_blocks(body, lo, hi)
+        return jnp.sum(squares[lo:hi, :], axis=1, keepdims=True)
 
     def mask_rows(r):
         row = r.start + lax.broadcasted_iota(jnp.int32, (ROW_BLOCK, cols), 0)
@@ -130,22 +151,15 @@
         values = kept[r, :].astype(jnp.float32)
         kept[r, :] = jnp.where(position < limit, values, 0.0).astype(jnp.bfloat16)
 
-    row_blocks(mask_rows)
-    loaded(up_load)
-    place(2, contract(kept[...], up[...], (1, 1)), None)
-    loaded(fwd_load)
-    place(0, contract(fwd[...], down[...], (1, 1)), squares_of(fwd))
-
-    sections = (sec + n_section - 1) // n_section + (2 * n_section - 2 - sec) // n_section
-    pl.semaphore_wait(barrier, n_tensor - 1 + 1 + n_z - 1 + sections)
-
-    @pl.when(sec == 0)
-    def _():
-        next_f[...] = jnp.zeros_like(next_f)
-
-    @pl.when(sec == n_section - 1)
-    def _():
-        next_g[...] = jnp.zeros_like(next_g)
+    def place(which, part, total, chunks):
+        base = chunks[0][0]
+        part = part.astype(jnp.bfloat16)
+        for r0, n in chunks:
+            at = 3 * r0 + which * n
+            own[at : at + n, :units] = part[r0 - base : r0 - base + n]
+            if total is not None:
+                spread = jnp.broadcast_to(total[r0 - base : r0 - base + n].astype(jnp.bfloat16), (n, 256 - units))
+                own[at : at + n, units:] = spread
 
     x_copies = []
     for c, (r0, n) in enumerate(CHUNKS):
@@ -154,13 +168,63 @@
             remote(own.at[at], others.at[k, at], x_send.at[c, k], x_recv.at[c, k], x_peers[k])
             for k in range(n_tensor - 1)
         ])
-        for copy in x_copies[-1]:
+
+    gain_load.wait()
+    gain_row = gain[...].astype(jnp.float32)
+
+    def scale_down(r):
+        down[r, :] = (down[r, :].astype(jnp.float32) * gain_row).astype(jnp.bfloat16)
+
+    head, rest = CHUNKS[:1], CHUNKS[1:]
+    loaded(down_load)
+    row_blocks(scale_down, 0, units)
+    loaded((saved_load[0], fwd_load[0]))
+    both = contract(jnp.concatenate([saved[:HEAD, :], fwd[:HEAD, :]], axis=0), down[...], (1, 1))
+    place(1, both[:HEAD], squares_of(saved, 0, HEAD), head)
+    place(0, both[HEAD:], squares_of(fwd, 0, HEAD), head)
+    loaded((kept_load[0], lens_load))
+    row_blocks(mask_rows, 0, HEAD)
+    loaded(up_load)
+    place(2, contract(kept[:HEAD, :], up[...], (1, 1)), None, head)
+    with jax.named_scope("near"):
+        meet_near()
+    for copy in x_copies[0]:
+        copy.start()
+
+    loaded(saved_load[1:])
+    place(1, contract(saved[HEAD:, :], down[...], (1, 1)), squares_of(saved, HEAD, rows), rest)
+    loaded(fwd_load[1:])
+    place(0, contract(fwd[HEAD:, :], down[...], (1, 1)), squares_of(fwd, HEAD, rows), rest)
+    loaded(kept_load[1:])
+    row_blocks(mask_rows, HEAD, rows)
+    place(2, contract(kept[HEAD:, :], up[...], (1, 1)), None, rest)
+    for copies in x_copies[1:]:
+        for copy in copies:
             copy.start()
 
+    @pl.when(sec == 0)
+    def _():
+        next_f[...] = jnp.zeros_like(next_f)
+
+    @pl.when(sec == n_section - 1)
+    def _():
+        next_g[...] = jnp.zeros_like(next_g)
+
     f_copies, b_copies = [], []
+
+    def send_rows(c):
+        @pl.when(has_prev)
+        def _():
+            b_copies[c].start()
+
+        @pl.when(has_next)
+        def _():
+            f_copies[c].start()
+
     for c, (r0, n) in enumerate(CHUNKS):
-        for copy in x_copies[c]:
-            copy.wait_recv()
+        with jax.named_scope(f"x{c}"):
+            for copy in x_copies[c]:
+                copy.wait_recv()
 
         def summed(which):
             at = pl.ds(3 * r0 + which * n, n)
@@ -188,23 +252,24 @@
             values = kept[r, t].astype(jnp.float32) + weighted - saved[r, t].astype(jnp.float32) * pull
             back_out[r, t] = values.astype(jnp.bfloat16)
 
-        col_tiles(back_tile)
+        col_tiles(back_tile, 2 if c else True)
         b_copies.append(remote(back_out.at[r], next_g.at[r], b_send.at[c], b_recv.at[c], {"section": sec - 1}))
-
-        @pl.when(has_prev)
-        def _():
-            b_copies[c].start()
 
         def fwd_tile(t):
             raised = contract(act, up[:, t], (1, 0))
             fwd_out[r, t] = (fwd[r, t].astype(jnp.float32) + raised).astype(jnp.bfloat16)
 
-        col_tiles(fwd_tile)
+        col_tiles(fwd_tile, 2 if c else True)
         f_copies.append(remote(fwd_out.at[r], next_f.at[r], f_send.at[c], f_recv.at[c], {"section": sec + 1}))
-
-        @pl.when(has_next)
-        def _():
-            f_copies[c].start()
+        if c == 0:
+            with jax.named_scope("sections"):
+                meet_sections()
+        if c < len(CHUNKS) - 1:
+            send_rows(c)
+        else:
+            @pl.when(jnp.logical_not(early))
+            def _():
+                send_rows(c)
 
     def part_tile(t):
         share = units // n_dp
@@ -215,7 +280,8 @@
             parts[i % 2, i // 2, 0, :, t] = down_part[at]
             parts[i % 2, i // 2, 1, :, t] = up_part[at]
 
-    col_tiles(part_tile)
+    with jax.named_scope("parts"):
+        col_tiles(part_tile)
     order = [lax.rem(z + k, n_z) for k in (*range(1, n_z), 0)]
     c_copies = []
     for i, at in enumerate(order):
@@ -223,7 +289,8 @@
         c_copies[-1].start()
     z_copies = []
     for i, at in enumerate(order):
-        c_copies[i].wait_recv()
+        with jax.named_scope(f"c{i}"):
+            c_copies[i].wait_recv()
 
         def add(t):
             for a in range(2):
@@ -235,8 +302,14 @@
         if i < n_z - 1:
             z_copies.append(remote(chip_sum.at[i], from_chip.at[i], z_send.at[i], z_recv.at[i], z_peers[i]))
             z_copies[-1].start()
-    for copy in z_copies:
-        copy.wait_recv()
+
+    @pl.when(early)
+    def _():
+        send_rows(len(CHUNKS) - 1)
+
+    with jax.named_scope("z"):
+        for copy in z_copies:
+            copy.wait_recv()
 
     def finish(t):
         for a in range(2):
@@ -250,18 +323,28 @@
     for copies in x_copies:
         for copy in copies:
             copy.wait_send()
-    for copy in (*c_copies, *z_copies):
-        copy.wait_send()
     for c in range(len(CHUNKS)):
-        @pl.when(has_prev)
-        def _():
-            b_copies[c].wait_send()
-            f_copies[c].wait_recv()
-
-        @pl.when(has_next)
-        def _():
-            f_copies[c].wait_send()
-            b_copies[c].wait_recv()
+        with jax.named_scope(f"f{c}"):
+            @pl.when(has_prev)
+            def _():
+                f_copies[c].wait_recv()
+
+        with jax.named_scope(f"b{c}"):
+            @pl.when(has_next)
+            def _():
+                b_copies[c].wait_recv()
+
+    with jax.named_scope("sent"):
+        for copy in (*c_copies, *z_copies):
+            copy.wait_send()
+        for c in range(len(CHUNKS)):
+            @pl.when(has_prev)
+            def _():
+                b_copies[c].wait_send()
+
+            @pl.when(has_next)
+            def _():
+                f_copies[c].wait_send()
 
 
 def put_out(*refs):
@@ -316,6 +399,7 @@
                 pltpu.VMEM((n_z - 1, 2, share, cols), bf16),
                 pltpu.SMEM((2,), jnp.int32),
                 pltpu.VMEM((1, cols), bf16),
+                *[pltpu.SemaphoreType.REGULAR] * 2,
                 dma((2,)),
                 dma((5, PIECES)),
                 *[dma((n, n_tensor - 1))] * 2,

time: 85.5 us -> 84.3 us (0.986)
  the two profiles are of different devices: /device:TPU:49 before, /device:TPU:1 now
where the time goes in v3:
time: 84.3 us; the launch traced here: 84.1 us
  Pallas kernels  83.5 us (99%)
    pallas_call x1, Pallas kernels, shards(): pl.pallas_call(functools.partial(kernel, n_section, n_tensor, n_dp), out_...  82.1 us

profile of v3, /device:TPU:1, one launch (start us, length us, event | category | flops | bytes accessed | tf_op | source)
XLA Modules:
  0.0 84.1 jit_solution(7801351188124905669)
XLA Ops:
  0.6 82.1 %shard_map.102 = (bf16[192,2048]{1,0:T(8,128)(2,1)S(1)}, bf16[192,2048]{1,0:T(8,128)(2,1)S(1)}, bf16[32,2048]{1,0:T(8,128)(2,1)S(1)}, bf16[32,2048]{1,0:T(8,128)(2,1)S(1)}) custom-call(s32[2]{0:T(128)} %bitcast.15, bf16[1,2048]{1,0:T(2,128)(2,1)} %gain_hbm.1, bf16[192,2048]{1,0:T(8,128)(2,1)} %bitcast.10, bf16[192,2048]{1,0:T(8,128)(2,1)} %bitcast.11, ...), custom_call_target="tpu_custom_call" | custom-call | tf_op jit(solution)/shard_map/pallas_call | solution.py:376
  82.8 1.3 %shard_map.103 = (bf16[192,2048]{1,0:T(8,128)(2,1)}, bf16[192,2048]{1,0:T(8,128)(2,1)}, bf16[32,2048]{1,0:T(8,128)(2,1)}, bf16[32,2048]{1,0:T(8,128)(2,1)}) custom-call(bf16[192,2048]{1,0:T(8,128)(2,1)S(1)} %get-tuple-element.12.refs_0_, bf16[192,2048]{1,0:T(8,128)(2,1)S(1)} %get-tuple-element.13.refs_1_, bf16[32,2048]{1,0:T(8,128)(2,1)S(1)} %get-tuple-element.14.refs_2_, ...), custom_call_target="tpu_custom_call" | custom-call | tf_op jit(solution)/shard_map/pallas_call | solution.py:422

commit v4 on v3

--- a/solution.py
+++ b/solution.py
@@ -33,7 +33,7 @@
     next_f, next_g, grad_down, grad_up,
     fwd, saved, kept, down, up, squares, fwd_out, back_out, own, others, sact_all, back_all,
     parts, from_core, chip_sum, from_chip,
-    lens, gain, near, far, small_sem, load_sem, x_send, x_recv, f_send, f_recv, b_send, b_recv, c_send, c_recv, z_send, z_recv,
+    lens, gain, near, far_next, far_prev, mate, small_sem, load_sem, x_send, x_recv, f_send, f_recv, b_send, b_recv, c_send, c_recv, z_send, z_recv,
 ):
     rows, cols = fwd.shape
     units = down.shape[0]
@@ -41,7 +41,8 @@
     sec, ten, dp = lax.axis_index("section"), lax.axis_index("tensor"), lax.axis_index("dp")
     n_z = n_dp // 2
     z, core = dp // 2, dp % 2
-    early = jnp.logical_and(lax.rem(sec, EARLY_EVERY) == 0, sec > 0)
+    early = lax.rem(sec, EARLY_EVERY) == 0
+    dp_first = jnp.logical_and(early, sec > 0)
     has_next, has_prev = sec < n_section - 1, sec > 0
 
     lens_load = pltpu.make_async_copy(lens_hbm, lens, small_sem.at[0])
@@ -74,47 +75,100 @@
     core_peer = {"dp": z * 2 + 1 - core}
     z_peers = [{"dp": lax.rem(z + k, n_z) * 2 + core} for k in range(1, n_z)]
     barrier = pltpu.get_barrier_semaphore()
-
-    def enter(peer):
-        pl.semaphore_signal(barrier, inc=1, device_id=peer, device_id_type=MESH)
-
-    for k in range(1, n_tensor):
-        enter({"tensor": lax.rem(ten + k, n_tensor), "dp": z * 2})
-    for k in range(1, n_z):
-        enter({"dp": lax.rem(z + k, n_z) * 2})
-
-    @pl.when(core == 1)
+    odd = lax.rem(ten, 2)
+    pair = ten - odd
+
+    def signal(sem, peer):
+        pl.semaphore_signal(sem, inc=1, device_id=peer, device_id_type=MESH)
+
+    def of_pair(place, which):
+        return {"tensor": pair + place, "dp": z * 2 + which}
+
+    even0, odd0, even1, odd1 = of_pair(0, 0), of_pair(1, 0), of_pair(0, 1), of_pair(1, 1)
+    is_even0, is_odd0, is_even1, is_odd1 = (
+        jnp.logical_and(odd == place, core == which) for which in range(2) for place in range(2)
+    )
+
+    for k in range(0, n_tensor, 2):
+        ear = {"tensor": lax.rem(pair + k, n_tensor) + core, "dp": z * 2}
+        if k:
+            signal(barrier, ear)
+        else:
+            @pl.when(jnp.logical_not(is_even0))
+            def _():
+                signal(barrier, ear)
+
+    @pl.when(has_prev)
     def _():
-        enter({"dp": z * 2})
+        signal(barrier, {"section": sec - 1, "tensor": pair, "dp": z * 2 + 1})
 
     @pl.when(has_next)
     def _():
-        enter({"section": sec + 1, "dp": z * 2 + 1})
-
-    @pl.when(has_prev)
-    def _():
-        enter({"section": sec - 1, "dp": z * 2 + 1})
+        signal(barrier, {"section": sec + 1, "tensor": pair + 1, "dp": z * 2 + 1})
+
+    for k in range(1, n_z):
+        signal(barrier, {"tensor": pair + 1, "dp": lax.rem(z + k, n_z) * 2 + 1})
+
+    def tell_near():
+        @pl.when(is_even0)
+        def _():
+            pl.semaphore_wait(barrier, n_tensor - 1)
+            signal(near, odd0)
+
+        @pl.when(is_odd0)
+        def _():
+            pl.semaphore_wait(barrier, n_tensor)
+            signal(near, even1)
+            signal(near, odd1)
 
     def meet_near():
-        @pl.when(core == 0)
-        def _():
-            pl.semaphore_wait(barrier, 2 * (n_tensor - 1) + 2 * (n_z - 1) + 1)
-            pl.semaphore_signal(near, inc=1, device_id=core_peer, device_id_type=MESH)
-
-        @pl.when(core == 1)
+        @pl.when(jnp.logical_not(is_even0))
         def _():
             pl.semaphore_wait(near, 1)
 
-    def meet_sections():
-        @pl.when(core == 1)
-        def _():
-            sections = (sec + n_section - 1) // n_section + (2 * n_section - 2 - sec) // n_section
-            pl.semaphore_wait(barrier, 2 * sections)
-            pl.semaphore_signal(far, inc=1, device_id=core_peer, device_id_type=MESH)
-
-        @pl.when(core == 0)
-        def _():
-            pl.semaphore_wait(far, 1)
+    def tell_next():
+        @pl.when(is_even1)
+        def _():
+            @pl.when(has_next)
+            def _():
+                pl.semaphore_wait(barrier, 4)
+
+            signal(far_next, odd0)
+            signal(far_next, odd1)
+
+    def meet_next():
+        @pl.when(jnp.logical_not(is_even1))
+        def _():
+            pl.semaphore_wait(far_next, 1)
+
+        @pl.when(is_odd0)
+        def _():
+            signal(far_next, even0)
+
+        @pl.when(is_even0)
+        def _():
+            signal(mate, even1)
+
+    def tell_prev():
+        @pl.when(is_odd1)
+        def _():
+            pl.semaphore_wait(barrier, 4 * ((sec + n_section - 1) // n_section) + 4 * (n_z - 1))
+            signal(far_prev, odd0)
+            signal(far_prev, even1)
+
+    def meet_prev():
+        @pl.when(jnp.logical_not(is_odd1))
+        def _():
+            pl.semaphore_wait(far_prev, 1)
+
+        @pl.when(is_odd0)
+        def _():
+            signal(far_prev, even0)
+
+    def meet_mate():
+        @pl.when(is_even1)
+        def _():
+            pl.semaphore_wait(mate, 1)
 
     def row_blocks(body, lo, hi):
         def step(i, carry):
@@ -176,15 +230,19 @@
         down[r, :] = (down[r, :].astype(jnp.float32) * gain_row).astype(jnp.bfloat16)
 
     head, rest = CHUNKS[:1], CHUNKS[1:]
-    loaded(down_load)
+    with jax.named_scope("ldd"):
+        loaded(down_load)
     row_blocks(scale_down, 0, units)
-    loaded((saved_load[0], fwd_load[0]))
+    with jax.named_scope("ldh"):
+        loaded((saved_load[0], fwd_load[0]))
     both = contract(jnp.concatenate([saved[:HEAD, :], fwd[:HEAD, :]], axis=0), down[...], (1, 1))
     place(1, both[:HEAD], squares_of(saved, 0, HEAD), head)
     place(0, both[HEAD:], squares_of(fwd, 0, HEAD), head)
+    tell_near()
     loaded((kept_load[0], lens_load))
     row_blocks(mask_rows, 0, HEAD)
-    loaded(up_load)
+    with jax.named_scope("ldu"):
+        loaded(up_load)
     place(2, contract(kept[:HEAD, :], up[...], (1, 1)), None, head)
     with jax.named_scope("near"):
         meet_near()
@@ -202,6 +260,13 @@
         for copy in copies:
             copy.start()
 
+    with jax.named_scope("tell"):
+        tell_next()
+
+        @pl.when(jnp.logical_not(early))
+        def _():
+            tell_prev()
+
     @pl.when(sec == 0)
     def _():
         next_f[...] = jnp.zeros_like(next_f)
@@ -212,11 +277,12 @@
 
     f_copies, b_copies = [], []
 
-    def send_rows(c):
+    def send_back(c):
         @pl.when(has_prev)
         def _():
             b_copies[c].start()
 
+    def send_fwd(c):
         @pl.when(has_next)
         def _():
             f_copies[c].start()
@@ -255,6 +321,17 @@
         col_tiles(back_tile, 2 if c else True)
         b_copies.append(remote(back_out.at[r], next_g.at[r], b_send.at[c], b_recv.at[c], {"section": sec - 1}))
 
+        if c == 0:
+            @pl.when(jnp.logical_not(early))
+            def _():
+                with jax.named_scope("prev"):
+                    meet_prev()
+                send_back(c)
+        elif c < len(CHUNKS) - 1:
+            @pl.when(jnp.logical_not(early))
+            def _():
+                send_back(c)
+
         def fwd_tile(t):
             raised = contract(act, up[:, t], (1, 0))
             fwd_out[r, t] = (fwd[r, t].astype(jnp.float32) + raised).astype(jnp.bfloat16)
@@ -262,14 +339,27 @@
         col_tiles(fwd_tile, 2 if c else True)
         f_copies.append(remote(fwd_out.at[r], next_f.at[r], f_send.at[c], f_recv.at[c], {"section": sec + 1}))
         if c == 0:
-            with jax.named_scope("sections"):
-                meet_sections()
+            with jax.named_scope("next"):
+                meet_next()
         if c < len(CHUNKS) - 1:
-            send_rows(c)
-        else:
-            @pl.when(jnp.logical_not(early))
-            def _():
-                send_rows(c)
+            send_fwd(c)
+        if c == 1:
+            @pl.when(early)
+            def _():
+                with jax.named_scope("prevlate"):
+                    tell_prev()
+                    meet_prev()
+                send_back(0)
+                send_back(1)
+        if c == 2:
+            @pl.when(early)
+            def _():
+                send_back(c)
+        if c == len(CHUNKS) - 1:
+            @pl.when(jnp.logical_not(dp_first))
+            def _():
+                send_back(c)
+                send_fwd(c)
 
     def part_tile(t):
         share = units // n_dp
@@ -282,6 +372,7 @@
 
     with jax.named_scope("parts"):
         col_tiles(part_tile)
+    meet_mate()
     order = [lax.rem(z + k, n_z) for k in (*range(1, n_z), 0)]
     c_copies = []
     for i, at in enumerate(order):
@@ -303,9 +394,10 @@
             z_copies.append(remote(chip_sum.at[i], from_chip.at[i], z_send.at[i], z_recv.at[i], z_peers[i]))
             z_copies[-1].start()
 
-    @pl.when(early)
+    @pl.when(dp_first)
     def _():
-        send_rows(len(CHUNKS) - 1)
+        send_back(len(CHUNKS) - 1)
+        send_fwd(len(CHUNKS) - 1)
 
     with jax.named_scope("z"):
         for copy in z_copies:
@@ -399,7 +491,7 @@
                 pltpu.VMEM((n_z - 1, 2, share, cols), bf16),
                 pltpu.SMEM((2,), jnp.int32),
                 pltpu.VMEM((1, cols), bf16),
-                *[pltpu.SemaphoreType.REGULAR] * 2,
+                *[pltpu.SemaphoreType.REGULAR] * 4,
                 dma((2,)),
                 dma((5, PIECES)),
                 *[dma((n, n_tensor - 1))] * 2,

time: 84.3 us -> 79.5 us (0.943)
  the two profiles are of different devices: /device:TPU:1 before, /device:TPU:192 now
where the time goes in v4:
time: 79.5 us; the launch traced here: 79.4 us
  Pallas kernels  78.7 us (99%)
    pallas_call x1, Pallas kernels, shards(): pl.pallas_call(functools.partial(kernel, n_section, n_tensor, n_dp), out_...  77.4 us

profile of v4, /device:TPU:192, one launch (start us, length us, event | category | flops | bytes accessed | tf_op | source)
XLA Modules:
  0.0 79.4 jit_solution(14267116392600248900)
XLA Ops:
  0.6 77.4 %shard_map.102 = (bf16[192,2048]{1,0:T(8,128)(2,1)S(1)}, bf16[192,2048]{1,0:T(8,128)(2,1)S(1)}, bf16[32,2048]{1,0:T(8,128)(2,1)S(1)}, bf16[32,2048]{1,0:T(8,128)(2,1)S(1)}) custom-call(s32[2]{0:T(128)} %bitcast.15, bf16[1,2048]{1,0:T(2,128)(2,1)} %gain_hbm.1, bf16[192,2048]{1,0:T(8,128)(2,1)} %bitcast.10, bf16[192,2048]{1,0:T(8,128)(2,1)} %bitcast.11, ...), custom_call_target="tpu_custom_call" | custom-call | tf_op jit(solution)/shard_map/pallas_call | solution.py:468
  78.0 1.3 %shard_map.103 = (bf16[192,2048]{1,0:T(8,128)(2,1)}, bf16[192,2048]{1,0:T(8,128)(2,1)}, bf16[32,2048]{1,0:T(8,128)(2,1)}, bf16[32,2048]{1,0:T(8,128)(2,1)}) custom-call(bf16[192,2048]{1,0:T(8,128)(2,1)S(1)} %get-tuple-element.12.refs_0_, bf16[192,2048]{1,0:T(8,128)(2,1)S(1)} %get-tuple-element.13.refs_1_, bf16[32,2048]{1,0:T(8,128)(2,1)S(1)} %get-tuple-element.14.refs_2_, ...), custom_call_target="tpu_custom_call" | custom-call | tf_op jit(solution)/shard_map/pallas_call | solution.py:514
